TPU v7x, 32 devices: a whole 2x2x4 slice. The times are simulated.
32 devices in a mesh: lat: 8 (over z, x), lon: 4 (over y, core).
Axes of the slice: x: 2, y: 2, z: 4, core: 2. Of those that a mesh axis runs over, the one named last changes fastest.
Arguments:
- fields: float32 [8, 8, 128, 512], P(None, None, 'lat', 'lon'), may hold values from -6 to 6
- ocean_mask: int32 [128, 4], replicated, may hold values from 0 to 1, as said below
- scale_table: float32 [16], replicated, may hold values from 0.5 to 4
- offset_table: float32 [16], replicated, may hold values from -4 to 4
- scale_index: int32 [8], replicated, may hold values from 0 to 15
- offset_index: int32 [8], replicated, may hold values from 0 to 15
Outputs:
- history: float32 [8, 8, 128, 512], P(None, 'lat', 'lon')
- record_range: float32 [2, 8, 8], P(None, None, 'lat')
Inputs may be any that keep to these rules, and one draw needn't show every extreme that they name: `ocean_mask`: each device's block of 16 rows and 128 longitudes holds at least half of 12 (rounded down, and never fewer than one) and at most 12 ocean strips; some block holds exactly 12.
All inputs are finite; a program needn't handle non-finite values.
Results may differ from a plain program's by a relative error of at most 0.00007.
Values sent between devices are 32-bit elements; how exact they have to be, the bound alone decides.
A program may use at most 64 MiB of HBM per device.

v0:
```python
import jax
import jax.numpy as jnp
from jax import lax
from jax.sharding import PartitionSpec as P

STRIP = 128


def per_device(fields, ocean_mask, scale_table, offset_table, scale_index, offset_index):
    nfield, level_count, lat_rows, lon_cells = fields.shape
    lat_count = lax.axis_size("lat")
    lon_count = lax.axis_size("lon")
    lat_pos = lax.axis_index("lat")
    lon_pos = lax.axis_index("lon")
    strips = lon_cells // STRIP
    slab_blocks = lat_count // lon_count
    table_slots = jnp.arange(scale_table.shape[0])
    scale_pick = scale_index[:, None] == table_slots[None, :]
    offset_pick = offset_index[:, None] == table_slots[None, :]
    scales = jnp.sum(jnp.where(scale_pick, scale_table[None, :], 0.0), axis=1)
    offsets = jnp.sum(jnp.where(offset_pick, offset_table[None, :], 0.0), axis=1)
    own_mask = lax.dynamic_slice(
        ocean_mask, (lat_pos * lat_rows, lon_pos * strips), (lat_rows, strips)
    )
    own_live = jnp.repeat(own_mask, STRIP, axis=1) > 0
    packed = (fields - offsets[:, None, None, None]) * scales[:, None, None, None]
    slab_mask = lax.dynamic_slice(
        ocean_mask,
        (lon_pos * slab_blocks * lat_rows, 0),
        (slab_blocks * lat_rows, lon_count * strips),
    )
    slab_live = jnp.repeat(slab_mask, STRIP, axis=1) > 0
    masked_block = jnp.where(own_live[None, None], packed, 0.0)
    history = lax.all_to_all(
        lax.all_to_all(masked_block, "lat", split_axis=1, concat_axis=2, tiled=True),
        "lon",
        split_axis=2,
        concat_axis=3,
        tiled=True,
    )
    highest = jnp.max(jnp.where(slab_live[None, None], history, -jnp.inf), axis=(2, 3))
    negated = jnp.max(jnp.where(slab_live[None, None], -history, -jnp.inf), axis=(2, 3))
    own_levels = lax.pmax(jnp.stack([highest, negated]), "lon")
    record_range = jnp.stack([own_levels[0], -own_levels[1]])
    return (history, record_range)


def solution(mesh):
    return jax.shard_map(
        per_device,
        mesh=mesh,
        in_specs=(P(None, None, "lat", "lon"), P(), P(), P(), P(), P()),
        out_specs=(P(None, "lat", "lon", None), P(None, None, "lat")),
        check_vma=False,
    )
```

profile of v0, /device:TPU:0, one launch (start us, length us, event | category | flops | bytes accessed | tf_op | source)
XLA Modules:
  0.0 46.4 jit_solution(1260978863947469488)
XLA Ops:
  0.6 0.0 copy-start
  0.6 0.7 %copy-done = s32[128,4]{0,1:T(4,128)S(1)} copy-done((s32[128,4]{0,1:T(4,128)S(1)}, s32[128,4]{0,1:T(4,128)}, u32[]{:S(2)}) %copy-start) | copy-done | bytes 2072
  1.3 0.0 copy-start.1
  1.3 0.0 copy-start.2
  1.3 0.0 copy-start.3
  1.3 0.0 copy-start.4
  1.3 0.1 compare_bitcast_fusion
  1.4 0.6 %copy-done.1 = f32[16]{0:T(128)S(1)} copy-done((f32[16]{0:T(128)S(1)}, f32[16]{0:T(128)}, u32[]{:S(2)}) %copy-start.1) | copy-done | bytes 88
  2.0 0.0 copy-done.2
  2.0 0.0 copy-done.3
  2.0 0.0 copy-done.4
  2.0 0.2 select_reduce_fusion.2
  2.2 1.3 %fusion.1 = f32[8,8,16,128]{3,2,0,1:T(8,128)S(1)} fusion(f32[8,8,16,128]{3,2,1,0:T(8,128)} %param.6, f32[8]{0:T(128)S(1)} %get-tuple-element.14, f32[8]{0:T(128)S(1)} %get-tuple-element.15, pred[16]{0:T(512)(128)(4,1)S(1)} %compare_bitcast_fusion), kind=kLoop, calls=%fused_computation.2 | loop fusion | flops 393216 | bytes 1048656 | tf_op jit(solution)/shard_map/jit(_where)/select_n | solution.py:33
  3.5 21.6 %all_to_all.30 = f32[8,8,16,128]{3,2,0,1:T(8,128)S(1)} all-to-all(f32[8,8,16,128]{3,2,0,1:T(8,128)S(1)} %fusion.1), channel_id=1, replica_groups=mesh['lat'=8,'lon'=4] {'lat'}, dimensions={1} | all-to-all | bytes 1048576 | tf_op jit(solution)/shard_map/all_to_all | solution.py:35
  25.2 1.1 %copy.23 = f32[8,1,128,128]{3,0,1,2:T(8,128)} copy(f32[8,1,128,128]{3,2,0,1:T(8,128)S(1)} %bitcast.12) | data formatting | bytes 1048576 | tf_op jit(solution)/shard_map/all_to_all | solution.py:35
  26.3 3.5 %all-to-all-start.1 = ((f32[8,1,128,128]{3,0,1,2:T(8,128)}), f32[8,1,128,128]{3,0,1,2:T(8,128)S(1)}, u32[]{:S(2)}, u32[]{:S(2)}) async-start(f32[8,1,128,128]{3,0,1,2:T(8,128)} %copy.23), calls=%async_computation.1 | async-start | bytes 1048576 | tf_op jit(solution)/shard_map/all_to_all | solution.py:34
  29.7 0.1 dynamic-slice_compare_fusion
  29.8 8.7 %all-to-all-done.1 = f32[8,1,128,128]{3,0,1,2:T(8,128)S(1)} async-done(((f32[8,1,128,128]{3,0,1,2:T(8,128)}), f32[8,1,128,128]{3,0,1,2:T(8,128)S(1)}, u32[]{:S(2)}, u32[]{:S(2)}) %all-to-all-start.1) | async-done | bytes 524320 | tf_op jit(solution)/shard_map/all_to_all | solution.py:34
  38.5 0.1 copy.24
  38.6 0.3 copy.25
  39.0 0.3 select_reduce_fusion.1
  39.3 0.8 %copy.26 = f32[8,1,32,512]{3,2,1,0:T(8,128)} copy(f32[8,1,32,512]{3,1,2,0:T(1,128)S(1)} %bitcast.11) | data formatting | bytes 1048576
  40.1 5.7 %pmax.7 = f32[2,8,1]{1,2,0:T(1,128)S(1)} all-reduce(f32[2,8,1]{1,2,0:T(1,128)S(1)} %pad_maximum_fusion), channel_id=1, replica_groups=mesh['lat'=8,'lon'=4] {'lon'}, use_global_device_ids=true, to_apply=%region_4.5 | all-reduce | flops 16 | bytes 128 | tf_op jit(solution)/shard_map/pmax | solution.py:43
  45.9 0.6 %pad_maximum_fusion.1 = f32[2,8,1]{1,2,0:T(1,128)} fusion(f32[1,8,1]{1,2,0:T(1,128)S(1)} %get-tuple-element.13, f32[1,8,1]{1,2,0:T(1,128)S(1)} %get-tuple-element.12), kind=kLoop, calls=%fused_computation.12 | loop fusion | flops 16 | bytes 128 | tf_op jit(solution)/shard_map/stack | solution.py:44
  (3 shorter events, 0.1 us)
Async XLA Ops:
  0.6 0.7 %copy-start = (s32[128,4]{0,1:T(4,128)S(1)}, s32[128,4]{0,1:T(4,128)}, u32[]{:S(2)}) copy-start(s32[128,4]{0,1:T(4,128)} %param.7) | copy-start | bytes 6148
  1.3 0.7 %copy-start.1 = (f32[16]{0:T(128)S(1)}, f32[16]{0:T(128)}, u32[]{:S(2)}) copy-start(f32[16]{0:T(128)} %param.8) | copy-start | bytes 196
  1.3 0.7 %copy-start.2 = (s32[8]{0:T(128)S(1)}, s32[8]{0:T(128)}, u32[]{:S(2)}) copy-start(s32[8]{0:T(128)} %param.10) | copy-start | bytes 100
  1.3 0.7 %copy-start.3 = (f32[16]{0:T(128)S(1)}, f32[16]{0:T(128)}, u32[]{:S(2)}) copy-start(f32[16]{0:T(128)} %param.9) | copy-start | bytes 196
  1.3 0.7 %copy-start.4 = (s32[8]{0:T(128)S(1)}, s32[8]{0:T(128)}, u32[]{:S(2)}) copy-start(s32[8]{0:T(128)} %param.11) | copy-start | bytes 100
  26.3 12.3 %all-to-all-start.1 = ((f32[8,1,128,128]{3,0,1,2:T(8,128)}), f32[8,1,128,128]{3,0,1,2:T(8,128)S(1)}, u32[]{:S(2)}, u32[]{:S(2)}) async-start(f32[8,1,128,128]{3,0,1,2:T(8,128)} %copy.23), calls=%async_computation.1 | async-start | bytes 1048576 | tf_op jit(solution)/shard_map/all_to_all | solution.py:34
where the time goes:
time: 46.7 us; the launch traced here: 46.4 us
  blocking collectives  27.3 us (58%)
  waiting for transfers between devices  8.7 us (19%)
  local copies, waits for them, and re-layouts  3.72 us (8%)
  starting transfers between devices  3.47 us (7%)
  other arithmetic  2.49 us (5%)
  between operations  0.7 us (1%)
    all_to_all x1, blocking collectives, per_device(): lax.all_to_all(masked_block, 'lat', split_axis=1, concat_axis=2, tiled=True)  21.6 us
    all_to_all x1, waiting for transfers between devices, per_device(): lax.all_to_all(lax.all_to_all(masked_block, 'lat', split_axis=1, concat_a...  8.7 us
    pmax x1, blocking collectives, per_device(): own_levels = lax.pmax(jnp.stack([highest, negated]), 'lon')  5.74 us
    all_to_all x1, starting transfers between devices, per_device(): lax.all_to_all(lax.all_to_all(masked_block, 'lat', split_axis=1, concat_a...  3.47 us
    unnamed x11, local copies, waits for them, and re-layouts  2.14 us
    select_n x1, other arithmetic, per_device(): masked_block = jnp.where(own_live[None, None], packed, 0.0)  1.26 us
    all_to_all x2, local copies, waits for them, and re-layouts, per_device(): lax.all_to_all(masked_block, 'lat', split_axis=1, concat_axis=2, tiled=True)  1.14 us
  transfers between devices with their start and end apart: 1, of which 1 were waited for; matrix products, arithmetic and copies ran while one was open for 0% of the time, Pallas kernels for 0%

commit v1 on v0

v1 whole, which is shorter than its diff:
```python
import functools

import jax
import jax.numpy as jnp
from jax import lax
from jax.experimental import pallas as pl
from jax.experimental.pallas import tpu as pltpu
from jax.sharding import PartitionSpec as P

STRIP = 128
MAX_LIVE = 12
MESH = pl.DeviceIdType.MESH


def kernel(
    dims, mask, scale_table, offset_table, scale_index, offset_index, x_hbm,
    out, rng,
    xv, send, recv, stage, part, stats, in_sem, send_sem, recv_sem, stat_send, stat_recv,
):
    fields, levels, rows, lat_count, lon_count = dims
    slab = lat_count // lon_count
    slots = send.shape[1]
    devices = lat_count * lon_count
    lat_pos = lax.axis_index("lat")
    lon_pos = lax.axis_index("lon")
    me = lat_pos * lon_count + lon_pos

    load = pltpu.make_async_copy(x_hbm, xv, in_sem)
    load.start()

    def peer(step):
        other = lax.rem(me + step, devices)
        return other // lon_count, lax.rem(other, lon_count)

    barrier = pltpu.get_barrier_semaphore()

    def greet(step, carry):
        pl.semaphore_signal(barrier, inc=1, device_id=peer(step), device_id_type=MESH)
        return carry

    lax.fori_loop(1, devices, greet, 0)

    seen = []
    total = jnp.int32(0)
    for r in range(rows):
        total = total + mask[lon_pos, lat_pos * rows + r]
        seen.append(total)
    picks = []
    for k in range(slots):
        slot = jnp.minimum(k, total - 1)
        pick = jnp.int32(0)
        for r in range(rows - 1):
            pick = pick + (seen[r] <= slot).astype(jnp.int32)
        picks.append(pick)

    which = lax.broadcasted_iota(jnp.int32, (fields, STRIP), 0)
    scales = jnp.zeros((fields, STRIP), jnp.float32)
    offsets = jnp.zeros((fields, STRIP), jnp.float32)
    for f in range(fields):
        scales = jnp.where(which == f, scale_table[scale_index[f]], scales)
        offsets = jnp.where(which == f, offset_table[offset_index[f]], offsets)

    load.wait()

    def pack(level, carry):
        high = None
        for k in range(slots):
            strip = xv[pl.ds(level * rows + picks[k], fields, stride=levels * rows), :]
            packed = (strip - offsets) * scales
            send[level, k] = packed
            high = packed if high is None else jnp.maximum(high, packed)
            low = -packed if k == 0 else jnp.maximum(low, -packed)
        part[pl.ds(pl.multiple_of(level * fields, fields), fields), :] = high
        part[pl.ds(pl.multiple_of((levels + level) * fields, fields), fields), :] = low
        return carry

    lax.fori_loop(0, levels, pack, 0)

    pl.semaphore_wait(barrier, devices - 1)

    slab_pos = lat_pos // slab
    here = lax.rem(lat_pos, slab) * lon_count + lon_pos

    def remote(level):
        return pltpu.make_async_remote_copy(
            src_ref=send.at[level],
            dst_ref=recv.at[here],
            send_sem=send_sem.at[level],
            recv_sem=recv_sem.at[here],
            device_id=(level, slab_pos),
            device_id_type=MESH,
        )

    def local(level):
        return pltpu.make_async_copy(send.at[level], recv.at[here], recv_sem.at[here])

    def is_self(level):
        return jnp.logical_and(level == lat_pos, slab_pos == lon_pos)

    def post(step, carry):
        level = lax.rem(lat_pos + lat_count // 2 + step, lat_count)

        @pl.when(is_self(level))
        def _():
            local(level).start()

        @pl.when(jnp.logical_not(is_self(level)))
        def _():
            remote(level).start()

        return carry

    lax.fori_loop(0, lat_count, post, 0)

    stat_rows = stats.shape[1]
    for j in range(stat_rows):
        tile = part[j * STRIP:(j + 1) * STRIP, :].T
        stats[me, j] = jnp.max(tile, axis=0, keepdims=True)

    def stat_copy(step):
        return pltpu.make_async_remote_copy(
            src_ref=stats.at[me],
            dst_ref=stats.at[me],
            send_sem=stat_send,
            recv_sem=stat_recv,
            device_id=peer(step),
            device_id_type=MESH,
        )

    def tell(step, carry):
        stat_copy(step).start()
        return carry

    lax.fori_loop(1, devices, tell, 0)

    per_field = (slab * rows) * lon_count

    for b in range(lon_count):
        for i in range(slab):
            source = i * lon_count + b
            pltpu.make_async_copy(recv.at[source], recv.at[source], recv_sem.at[source]).wait()
            stage[source] = recv[source]
            rank = jnp.int32(0)
            for r in range(rows):
                live = mask[b, (lon_pos * slab + i) * rows + r]
                strip = stage[source, jnp.minimum(rank, slots - 1)]
                strip = jnp.where(live > 0, strip, 0.0)
                row = i * rows + r
                start = (row // 8 * lon_count + b) * 8 + row % 8
                out[pl.ds(start, fields, stride=per_field), :] = strip
                rank = rank + live

    others = stats.at[pl.ds(0, devices - 1)]
    pltpu.make_async_copy(others, others, stat_recv).wait()
    for end in range(2):
        first = (end * levels + lat_pos) * fields
        best = jnp.max(stats[:, first // STRIP], axis=0)
        best = jnp.broadcast_to(best, (8, STRIP))
        own = pltpu.roll(best, lax.rem(STRIP - lax.rem(first, STRIP), STRIP), 1)
        own = own[:1, :fields]
        rng[end] = own if end == 0 else -own

    def drain(step, carry):
        level = lax.rem(lat_pos + step, lat_count)

        @pl.when(jnp.logical_not(is_self(level)))
        def _():
            remote(level).wait_send()

        return carry

    lax.fori_loop(0, lat_count, drain, 0)
    pltpu.make_async_copy(others, others, stat_send).wait()


def per_device(fields, ocean_mask, scale_table, offset_table, scale_index, offset_index):
    nfield, levels, rows, cells = fields.shape
    lat_count = lax.axis_size("lat")
    lon_count = lax.axis_size("lon")
    slab = lat_count // lon_count
    devices = lat_count * lon_count
    slots = min(MAX_LIVE, rows)
    sources = slab * lon_count
    out_rows = nfield * slab * rows * lon_count
    smem = pl.BlockSpec(memory_space=pltpu.SMEM)
    vmem = pl.BlockSpec(memory_space=pltpu.VMEM)
    history, record_range = pl.pallas_call(
        functools.partial(kernel, (nfield, levels, rows, lat_count, lon_count)),
        out_shape=(
            jax.ShapeDtypeStruct((out_rows, STRIP), jnp.float32),
            jax.ShapeDtypeStruct((2, 1, nfield), jnp.float32),
        ),
        in_specs=[smem] * 5 + [pl.BlockSpec(memory_space=pl.ANY)],
        out_specs=(vmem, vmem),
        scratch_shapes=[
            pltpu.VMEM((nfield * levels * rows, STRIP), jnp.float32),
            pltpu.VMEM((levels, slots, nfield, STRIP), jnp.float32),
            pltpu.VMEM((sources, slots, nfield, STRIP), jnp.float32),
            pltpu.VMEM((sources, slots, nfield, STRIP), jnp.float32),
            pltpu.VMEM((2 * levels * nfield, STRIP), jnp.float32),
            pltpu.VMEM((devices, 2 * levels * nfield // STRIP, 1, STRIP), jnp.float32),
            pltpu.SemaphoreType.DMA,
            pltpu.SemaphoreType.DMA((levels,)),
            pltpu.SemaphoreType.DMA((sources,)),
            pltpu.SemaphoreType.DMA,
            pltpu.SemaphoreType.DMA,
        ],
        compiler_params=pltpu.CompilerParams(collective_id=0, has_side_effects=True),
    )(
        ocean_mask.T, scale_table, offset_table, scale_index, offset_index,
        fields.reshape(nfield * levels * rows, cells),
    )
    history = history.reshape(nfield, slab * rows // 8, lon_count, 8, STRIP)
    history = history.transpose(0, 1, 3, 2, 4)
    return history.reshape(nfield, 1, slab * rows, lon_count * STRIP), record_range.reshape(2, nfield, 1)


def solution(mesh):
    return jax.shard_map(
        per_device,
        mesh=mesh,
        in_specs=(P(None, None, "lat", "lon"), P(), P(), P(), P(), P()),
        out_specs=(P(None, "lat", "lon", None), P(None, None, "lat")),
        check_vma=False,
    )
```

time: 46.7 us -> 22.9 us (0.49)
  blocking collectives: 27.3 us -> 0 us
  Pallas kernels: 0 us -> 19.6 us
  waiting for transfers between devices: 8.7 us -> 0 us
  starting transfers between devices: 3.47 us -> 0 us
  other arithmetic: 2.49 us -> 0 us
  local copies, waits for them, and re-layouts: 3.72 us -> 2.44 us
    all_to_all x1 -> x0, blocking collectives: 21.6 us -> none  [per_device(): lax.all_to_all(masked_block, 'lat', split_axis=1, concat_axis=2, tiled=True)]
    pallas_call x0 -> x1, Pallas kernels: none -> 19.6 us  [per_device(): pl.pallas_call(functools.partial(kernel, (nfield, levels, rows, lat_count...]
    all_to_all x1 -> x0, waiting for transfers between devices: 8.7 us -> none  [per_device(): lax.all_to_all(lax.all_to_all(masked_block, 'lat', split_axis=1, concat_a...]
    pmax x1 -> x0, blocking collectives: 5.74 us -> none  [per_device(): own_levels = lax.pmax(jnp.stack([highest, negated]), 'lon')]
    all_to_all x1 -> x0, starting transfers between devices: 3.47 us -> none  [per_device(): lax.all_to_all(lax.all_to_all(masked_block, 'lat', split_axis=1, concat_a...]
    all_to_all x4 -> x0, local copies, waits for them, and re-layouts: 1.59 us -> none  [the longest x2 1.14 us: per_device(): lax.all_to_all(masked_block, 'lat', split_axis=1, concat_axis=2, tiled=True)]
    select_n x1 -> x0, other arithmetic: 1.26 us -> none  [per_device(): masked_block = jnp.where(own_live[None, None], packed, 0.0)]
    another operation x2 -> x0, other arithmetic: 0.57 us -> none  [the longest x1 0.57 us: per_device(): record_range = jnp.stack([own_levels[0], -own_levels[1]])]
  transfers between devices with their start and end apart: 1 -> 0, of which waited for: 1 -> 0; matrix products, arithmetic and copies ran while one was open for 0% -> 0% of each run, Pallas kernels for 0% -> 0%
where the time goes in v1:
time: 22.9 us; the launch traced here: 22.7 us
  Pallas kernels  19.6 us (86%)
  local copies, waits for them, and re-layouts  2.44 us (11%)
  between operations  0.65 us (3%)
    pallas_call x1, Pallas kernels, per_device(): pl.pallas_call(functools.partial(kernel, (nfield, levels, rows, lat_count...  19.6 us
    unnamed x4, local copies, waits for them, and re-layouts  2.44 us

profile of v1, /device:TPU:0, one launch (start us, length us, event | category | flops | bytes accessed | tf_op | source)
XLA Modules:
  0.0 22.7 jit_solution(749410149425562223)
XLA Ops:
  0.6 19.6 %shard_map.77 = (f32[1024,128]{1,0:T(8,128)}, f32[2,1,8]{2,1,0:T(1,128)}) custom-call(s32[4,128]{1,0:T(4,128)} %bitcast.12, f32[16]{0:T(128)} %scale_table.1, f32[16]{0:T(128)} %offset_table.1, s32[8]{0:T(128)} %scale_index.1, s32[8]{0:T(128)} %offset_index.1, f32[1024,128]{1,0:T(8,128)} %bitcast.10), custom_call_target="tpu_custom_call" | custom-call | tf_op jit(solution)/shard_map/pallas_call | solution.py:187
  20.3 0.0 copy-start
  20.3 1.9 %copy.11 = f32[8,1,32,512]{3,2,1,0:T(8,128)} copy(f32[8,1,32,512]{3,2,1,0:T(8,128)} %bitcast.11) | data formatting | bytes 1048576
  22.1 0.0 copy-done
  22.1 0.6 %copy.12 = f32[2,8,1]{1,2,0:T(1,128)} copy(f32[2,8,1]{1,2,0:T(1,128)S(1)} %bitcast.13) | data formatting | bytes 128
Async XLA Ops:
  20.3 1.9 %copy-start = (f32[2,1,8]{2,1,0:T(1,128)S(1)}, f32[2,1,8]{2,1,0:T(1,128)}, u32[]{:S(2)}) copy-start(f32[2,1,8]{2,1,0:T(1,128)} %get-tuple-element.5) | copy-start | bytes 196

commit v2 on v1

v2 whole, which is shorter than its diff:
```python
import functools

import jax
import jax.numpy as jnp
from jax import lax
from jax.experimental import pallas as pl
from jax.experimental.pallas import tpu as pltpu
from jax.sharding import PartitionSpec as P

STRIP = 128
MAX_LIVE = 12
MESH = pl.DeviceIdType.MESH


def kernel(
    dims, mask_hbm, scale_table_hbm, offset_table_hbm, scale_index_hbm, offset_index_hbm, x_hbm,
    out, rng,
    mask, scale_table, offset_table, scale_index, offset_index,
    xv, send, recv, stage, part, first_stats, last_stats,
    in_sem, send_sem, recv_sem, stat_send, stat_recv, last_send, last_recv, from_below, from_above,
):
    fields, levels, rows, lat_count, lon_count = dims
    slab = lat_count // lon_count
    planes = lat_count // slab
    plane_size = slab * lon_count
    slots = send.shape[1]
    lat_pos = lax.axis_index("lat")
    lon_pos = lax.axis_index("lon")
    plane = lat_pos // slab
    here = lax.rem(lat_pos, slab) * lon_count + lon_pos

    barrier = pltpu.get_barrier_semaphore()

    def greet(step, carry):
        other = lax.rem(here + step, plane_size)
        target = (plane * slab + other // lon_count, lax.rem(other, lon_count))
        pl.semaphore_signal(barrier, inc=1, device_id=target, device_id_type=MESH)
        return carry

    lax.fori_loop(1, plane_size, greet, 0)
    has_above = plane < planes - 1
    has_below = plane > 0

    def call_above(sem):
        @pl.when(has_above)
        def _():
            pl.semaphore_signal(sem, inc=1, device_id=(lat_pos + slab, lon_pos), device_id_type=MESH)

    def call_below(sem):
        @pl.when(has_below)
        def _():
            pl.semaphore_signal(sem, inc=1, device_id=(lat_pos - slab, lon_pos), device_id_type=MESH)

    call_above(barrier)
    call_below(barrier)

    load = pltpu.make_async_copy(x_hbm, xv, in_sem.at[0])
    smalls = [
        pltpu.make_async_copy(src, dst, in_sem.at[n + 1])
        for n, (src, dst) in enumerate([
            (mask_hbm, mask), (scale_table_hbm, scale_table), (offset_table_hbm, offset_table),
            (scale_index_hbm, scale_index), (offset_index_hbm, offset_index),
        ])
    ]
    for copy in smalls:
        copy.start()
    load.start()
    for copy in smalls:
        copy.wait()

    seen = []
    total = jnp.int32(0)
    for r in range(rows):
        total = total + mask[lon_pos, lat_pos * rows + r]
        seen.append(total)
    picks = []
    for k in range(slots):
        slot = jnp.minimum(k, total - 1)
        pick = jnp.int32(0)
        for r in range(rows - 1):
            pick = pick + (seen[r] <= slot).astype(jnp.int32)
        picks.append(pick)

    which = lax.broadcasted_iota(jnp.int32, (fields, STRIP), 0)
    scales = jnp.zeros((fields, STRIP), jnp.float32)
    offsets = jnp.zeros((fields, STRIP), jnp.float32)
    for f in range(fields):
        scales = jnp.where(which == f, scale_table[scale_index[f]], scales)
        offsets = jnp.where(which == f, offset_table[offset_index[f]], offsets)

    load.wait()

    def pack(level, carry):
        high = None
        for k in range(slots):
            strip = xv[pl.ds(level * rows + picks[k], fields, stride=levels * rows), :]
            packed = (strip - offsets) * scales
            send[level, k] = packed
            high = packed if k == 0 else jnp.maximum(high, packed)
            low = -packed if k == 0 else jnp.maximum(low, -packed)
        part[pl.ds(pl.multiple_of(level * fields, fields), fields), :] = high
        part[pl.ds(pl.multiple_of((levels + level) * fields, fields), fields), :] = low
        return carry

    lax.fori_loop(0, levels, pack, 0)

    neighbours = has_above.astype(jnp.int32) + has_below.astype(jnp.int32)
    pl.semaphore_wait(barrier, plane_size - 1 + neighbours)
    call_above(from_below)
    call_below(from_above)

    for j in range(first_stats.shape[1]):
        tile = part[j * STRIP:(j + 1) * STRIP, :].T
        first_stats[plane, j] = jnp.max(tile, axis=0, keepdims=True)

    def remote(level):
        return pltpu.make_async_remote_copy(
            src_ref=send.at[level],
            dst_ref=recv.at[here],
            send_sem=send_sem.at[level],
            recv_sem=recv_sem.at[here],
            device_id=(level, plane),
            device_id_type=MESH,
        )

    def tell(target):
        return pltpu.make_async_remote_copy(
            src_ref=first_stats.at[plane],
            dst_ref=first_stats.at[plane],
            send_sem=stat_send.at[target],
            recv_sem=stat_recv.at[plane],
            device_id=(target * slab + lax.rem(lat_pos, slab), lon_pos),
            device_id_type=MESH,
        )

    def is_self(level):
        return jnp.logical_and(level == lat_pos, plane == lon_pos)

    for i in range(slab):
        level = plane * slab + i

        @pl.when(is_self(level))
        def _():
            pltpu.make_async_copy(send.at[level], recv.at[here], recv_sem.at[here]).start()

        @pl.when(jnp.logical_not(is_self(level)))
        def _():
            remote(level).start()

    def pass_from_below():
        pl.semaphore_wait(from_below, 1)
        call_above(from_below)

    def pass_from_above():
        pl.semaphore_wait(from_above, 1)
        call_below(from_above)

    def post_plane(target):
        for i in range(slab):
            remote(target * slab + i).start()

    def loop(low, high, body):
        def step(n, carry):
            body(n)
            return carry

        lax.fori_loop(low, high, step, 0)

    lower = plane < planes // 2

    @pl.when(lower)
    def _():
        loop(0, plane, lambda n: pass_from_below())
        loop(0, plane, lambda n: tell(n).start())

        def up(n):
            pass_from_above()
            tell(n).start()
            post_plane(n)

        loop(plane + 1, planes, up)
        loop(0, plane, post_plane)

    @pl.when(jnp.logical_not(lower))
    def _():
        loop(plane + 1, planes, lambda n: pass_from_above())
        loop(0, plane, lambda n: pass_from_below())
        loop(0, plane, lambda n: tell(n).start())
        loop(plane + 1, planes, lambda n: tell(n).start())
        loop(0, plane, post_plane)
        loop(plane + 1, planes, post_plane)

    def others(n, body):
        @pl.when(n != plane)
        def _():
            body(n)

    loop(0, planes, lambda n: others(n, lambda m: pltpu.make_async_copy(
        first_stats.at[m], first_stats.at[m], stat_recv.at[m]).wait()))
    last_stats[here] = jnp.max(first_stats[...], axis=0)

    def share(step):
        other = lax.rem(here + step, plane_size)
        return pltpu.make_async_remote_copy(
            src_ref=last_stats.at[here],
            dst_ref=last_stats.at[here],
            send_sem=last_send.at[step],
            recv_sem=last_recv.at[step],
            device_id=(plane * slab + other // lon_count, lax.rem(other, lon_count)),
            device_id_type=MESH,
        )

    loop(1, plane_size, lambda n: share(n).start())

    per_field = (slab * rows) * lon_count

    for b in range(lon_count):
        for i in range(slab):
            source = i * lon_count + b
            pltpu.make_async_copy(recv.at[source], recv.at[source], recv_sem.at[source]).wait()
            stage[source] = recv[source]
            rank = jnp.int32(0)
            for r in range(rows):
                live = mask[b, (lon_pos * slab + i) * rows + r]
                strip = stage[source, jnp.minimum(rank, slots - 1)]
                strip = jnp.where(live > 0, strip, 0.0)
                line = i * rows + r
                start = (line // 8 * lon_count + b) * 8 + line % 8
                out[pl.ds(start, fields, stride=per_field), :] = strip
                rank = rank + live

    loop(1, plane_size, lambda n: share(n).wait())
    for end in range(2):
        first = (end * levels + lat_pos) * fields
        best = jnp.max(last_stats[:, first // STRIP], axis=0)
        best = jnp.broadcast_to(best, (8, STRIP))
        own = pltpu.roll(best, lax.rem(STRIP - lax.rem(first, STRIP), STRIP), 1)
        own = own[:1, :fields]
        rng[end] = own if end == 0 else -own

    def drain(level, carry):
        @pl.when(jnp.logical_not(is_self(level)))
        def _():
            remote(level).wait_send()

        return carry

    lax.fori_loop(0, lat_count, drain, 0)
    loop(0, planes, lambda n: others(n, lambda m: tell(m).wait_send()))


def per_device(fields, ocean_mask, scale_table, offset_table, scale_index, offset_index):
    nfield, levels, rows, cells = fields.shape
    lat_count = lax.axis_size("lat")
    lon_count = lax.axis_size("lon")
    slab = lat_count // lon_count
    slots = min(MAX_LIVE, rows)
    sources = slab * lon_count
    out_rows = nfield * slab * rows * lon_count
    hbm = pl.BlockSpec(memory_space=pltpu.HBM)
    stat_rows = 2 * levels * nfield // STRIP
    vmem = pl.BlockSpec(memory_space=pltpu.VMEM)
    history, record_range = pl.pallas_call(
        functools.partial(kernel, (nfield, levels, rows, lat_count, lon_count)),
        out_shape=(
            jax.ShapeDtypeStruct((out_rows, STRIP), jnp.float32),
            jax.ShapeDtypeStruct((2, 1, nfield), jnp.float32),
        ),
        in_specs=[hbm] * 6,
        out_specs=(vmem, vmem),
        scratch_shapes=[
            pltpu.SMEM((lon_count, lat_count * rows), jnp.int32),
            pltpu.SMEM(scale_table.shape, jnp.float32),
            pltpu.SMEM(offset_table.shape, jnp.float32),
            pltpu.SMEM(scale_index.shape, jnp.int32),
            pltpu.SMEM(offset_index.shape, jnp.int32),
            pltpu.VMEM((nfield * levels * rows, STRIP), jnp.float32),
            pltpu.VMEM((levels, slots, nfield, STRIP), jnp.float32),
            pltpu.VMEM((sources, slots, nfield, STRIP), jnp.float32),
            pltpu.VMEM((sources, slots, nfield, STRIP), jnp.float32),
            pltpu.VMEM((2 * levels * nfield, STRIP), jnp.float32),
            pltpu.VMEM((lat_count // slab, stat_rows, 1, STRIP), jnp.float32),
            pltpu.VMEM((sources, stat_rows, 1, STRIP), jnp.float32),
            pltpu.SemaphoreType.DMA((6,)),
            pltpu.SemaphoreType.DMA((levels,)),
            pltpu.SemaphoreType.DMA((sources,)),
            pltpu.SemaphoreType.DMA((lat_count // slab,)),
            pltpu.SemaphoreType.DMA((lat_count // slab,)),
            pltpu.SemaphoreType.DMA((sources,)),
            pltpu.SemaphoreType.DMA((sources,)),
            pltpu.SemaphoreType.REGULAR,
            pltpu.SemaphoreType.REGULAR,
        ],
        compiler_params=pltpu.CompilerParams(
            collective_id=0, has_side_effects=True
        ),
    )(
        ocean_mask.T, scale_table, offset_table, scale_index, offset_index,
        fields.reshape(nfield * levels * rows, cells),
    )
    history = history.reshape(nfield, slab * rows // 8, lon_count, 8, STRIP)
    history = history.transpose(0, 1, 3, 2, 4)
    return history.reshape(nfield, 1, slab * rows, lon_count * STRIP), record_range.reshape(2, nfield, 1)


def solution(mesh):
    return jax.shard_map(
        per_device,
        mesh=mesh,
        in_specs=(P(None, None, "lat", "lon"), P(), P(), P(), P(), P()),
        out_specs=(P(None, "lat", "lon", None), P(None, None, "lat")),
        check_vma=False,
    )
```

time: 22.9 us -> 20.1 us (0.88)
  the two profiles are of different devices: /device:TPU:0 before, /device:TPU:14 now
where the time goes in v2:
time: 20.1 us; the launch traced here: 20 us
  Pallas kernels  16.9 us (84%)
  local copies, waits for them, and re-layouts  2.44 us (12%)
  between operations  0.65 us (3%)
    pallas_call x1, Pallas kernels, per_device(): pl.pallas_call(functools.partial(kernel, (nfield, levels, rows, lat_count...  16.9 us
    unnamed x4, local copies, waits for them, and re-layouts  2.44 us

profile of v2, /device:TPU:14, one launch (start us, length us, event | category | flops | bytes accessed | tf_op | source)
XLA Modules:
  0.0 20.0 jit_solution(6042078273437146195)
XLA Ops:
  0.6 16.9 %shard_map.77 = (f32[1024,128]{1,0:T(8,128)}, f32[2,1,8]{2,1,0:T(1,128)}) custom-call(s32[4,128]{1,0:T(4,128)} %bitcast.12, f32[16]{0:T(128)} %scale_table_hbm.1, f32[16]{0:T(128)} %offset_table_hbm.1, s32[8]{0:T(128)} %scale_index_hbm.1, s32[8]{0:T(128)} %offset_index_hbm.1, f32[1024,128]{1,0:T(8,128)} %bitcast.10), custom_call_target="tpu_custom_call" | custom-call | tf_op jit(solution)/shard_map/pallas_call | solution.py:263
  17.5 0.0 copy-start
  17.6 1.9 %copy.11 = f32[8,1,32,512]{3,2,1,0:T(8,128)} copy(f32[8,1,32,512]{3,2,1,0:T(8,128)} %bitcast.11) | data formatting | bytes 1048576
  19.4 0.0 copy-done
  19.4 0.6 %copy.12 = f32[2,8,1]{1,2,0:T(1,128)} copy(f32[2,8,1]{1,2,0:T(1,128)S(1)} %bitcast.13) | data formatting | bytes 128
Async XLA Ops:
  17.5 1.9 %copy-start = (f32[2,1,8]{2,1,0:T(1,128)S(1)}, f32[2,1,8]{2,1,0:T(1,128)}, u32[]{:S(2)}) copy-start(f32[2,1,8]{2,1,0:T(1,128)} %get-tuple-element.5) | copy-start | bytes 196
